TPU v7x, 32 devices: a whole 2x2x4 slice. The times are simulated.
32 devices in a mesh: ep: 8 (over y, x, core), tp: 4 (over z).
Axes of the slice: x: 2, y: 2, z: 4, core: 2. Of those that a mesh axis runs over, the one named last changes fastest.
Arguments:
- tokens: bfloat16 [4096, 2048], P('ep'), may hold values from -6 to 6
- lengths: int32 [8], P('ep'), may hold values from 256 to 512, as said below
- routes: int32 [4096, 4], P('ep'), may hold values from 0 to 7, all different within a row; in each aligned block of 512 rows (0 to 511, 512 to 1023, ...) at most 384 rows name the same one
- attention_gain: bfloat16 [2048], P('ep'), may hold values from 0.5 to 1.5
- query_weight: bfloat16 [2048, 2048], P('ep', 'tp'), may hold values from -0.125 to 0.125
- key_weight: bfloat16 [2048, 2048], P('ep', 'tp'), may hold values from -0.125 to 0.125
- value_weight: bfloat16 [2048, 2048], P('ep', 'tp'), may hold values from -0.125 to 0.125
- query_bias: bfloat16 [16, 128], P('tp', 'ep'), may hold values from -0.59765625 to 0.59765625
- key_bias: bfloat16 [16, 128], P('tp', 'ep'), may hold values from -0.59765625 to 0.59765625
- value_bias: bfloat16 [16, 128], P('tp', 'ep'), may hold values from -0.59765625 to 0.59765625
- output_weight: bfloat16 [2048, 2048], P('tp', 'ep'), may hold values from -0.5 to 0.5
- feedforward_gain: bfloat16 [2048], P('ep'), may hold values from 0.5 to 1.5
- router_weight: bfloat16 [2048, 8], P('ep'), may hold values from -0.0625 to 0.0625
- shared_switch: bfloat16 [2048], P('ep'), may hold values from -0.125 to 0.125
- shared_gate: bfloat16 [2048, 5632], P('ep', 'tp'), may hold values from -0.125 to 0.125
- shared_up: bfloat16 [2048, 5632], P('ep', 'tp'), may hold values from -0.125 to 0.125
- shared_down: bfloat16 [5632, 2048], P('tp', 'ep'), may hold values from -0.21875 to 0.21875
- expert_gate: bfloat16 [8, 2048, 1408], P('ep', None, 'tp'), may hold values from -0.125 to 0.125
- expert_up: bfloat16 [8, 2048, 1408], P('ep', None, 'tp'), may hold values from -0.125 to 0.125
- expert_down: bfloat16 [8, 1408, 2048], P('ep', 'tp'), may hold values from -1.25 to 1.25
- cotangent: bfloat16 [4096, 2048], P('ep'), may hold values from -6 to 6
Outputs:
- output: bfloat16 [4096, 2048], P('ep')
- aux_loss: float32 [], replicated
- expert_load: float32 [8], replicated
- tokens_grad: float32 [4096, 2048], P('ep')
- attention_gain_grad: float32 [2048], P('ep')
- query_weight_grad: float32 [2048, 2048], P('ep', 'tp')
- key_weight_grad: float32 [2048, 2048], P('ep', 'tp')
- value_weight_grad: float32 [2048, 2048], P('ep', 'tp')
- query_bias_grad: float32 [16, 128], P('tp', 'ep')
- key_bias_grad: float32 [16, 128], P('tp', 'ep')
- value_bias_grad: float32 [16, 128], P('tp', 'ep')
- output_weight_grad: float32 [2048, 2048], P('tp', 'ep')
- feedforward_gain_grad: float32 [2048], P('ep')
- router_weight_grad: float32 [2048, 8], P('ep')
- shared_switch_grad: float32 [2048], P('ep')
- shared_gate_grad: float32 [2048, 5632], P('ep', 'tp')
- shared_up_grad: float32 [2048, 5632], P('ep', 'tp')
- shared_down_grad: float32 [5632, 2048], P('tp', 'ep')
- expert_gate_grad: float32 [8, 2048, 1408], P('ep', None, 'tp')
- expert_up_gradient: float32 [8, 2048, 1408], P('ep', None, 'tp')
- expert_down_grad: float32 [8, 1408, 2048], P('ep', 'tp')
Inputs may be any that keep to these rules, and one draw needn't show every extreme that they name: `lengths`: every sequence has at least 256 tokens in use; in every draw one sequence is full and one has exactly 256. `routes`: A token names 4 different experts; among the 512 tokens of one sequence no expert is named more than 384 times, and in every draw some expert is named exactly 384 times by some sequence.
All inputs are finite; a program needn't handle non-finite values.
Results may differ from a plain program's by a relative error of at most 0.028.
Values may be sent and summed in bfloat16 or wider, within the bound.
A program may use at most 256 MiB of HBM per device.

v0:
```python
import jax
import jax.numpy as jnp
from jax import lax
from jax.sharding import PartitionSpec as P

epsilon = 1e-06
rope_base = 1000000.0
aux_weight = 0.001


def rotation_tables(slot_count, head_size):
    half_size = head_size // 2
    frequency = rope_base ** (-jnp.arange(half_size, dtype=jnp.float32) * 2.0 / head_size)
    angles = jnp.arange(slot_count, dtype=jnp.float32)[:, None] * frequency[None, :]
    cosine = jnp.concatenate([jnp.cos(angles), jnp.cos(angles)], -1)[:, None, :]
    sine_table = jnp.concatenate([jnp.sin(angles), jnp.sin(angles)], -1)[:, None, :]
    return (cosine, sine_table)


def rotate(values, cosine, sine_table):
    half_size = values.shape[-1] // 2
    turned = jnp.concatenate([-values[..., half_size:], values[..., :half_size]], -1)
    return values * cosine + turned * sine_table


def rotate_back(gradient, cosine, sine_table):
    half_size = gradient.shape[-1] // 2
    scaled = gradient * sine_table
    turned = jnp.concatenate([scaled[..., half_size:], -scaled[..., :half_size]], -1)
    return gradient * cosine + turned


def silu_parts(values):
    logistic_vals = lax.logistic(values)
    return (values * logistic_vals, logistic_vals * (1.0 + values * (1.0 - logistic_vals)))


def join_features(arrived):
    return lax.all_gather(arrived, "tp", axis=2, tiled=True)


def send_rows(buffer):
    return lax.all_to_all(buffer, "ep", split_axis=0, concat_axis=0, tiled=True)


def send_home(partial_value):
    summed_rows = lax.psum_scatter(partial_value, "tp", scatter_dimension=2, tiled=True).astype(
        jnp.bfloat16
    )
    arrived = lax.all_to_all(summed_rows, "ep", split_axis=0, concat_axis=0, tiled=True)
    return join_features(arrived)


def shards(
    tokens,
    lengths,
    routes,
    attention_gain,
    query_weight,
    key_weight,
    value_weight,
    query_bias,
    key_bias,
    value_bias,
    output_weight,
    feedforward_gain,
    router_weight,
    shared_switch,
    shared_gate,
    shared_up,
    shared_down,
    expert_gate,
    expert_up,
    expert_down,
    cotangent,
):
    single_float32 = jnp.float32
    brain_float16 = jnp.bfloat16
    (
        attention_gain,
        query_weight,
        key_weight,
        value_weight,
        query_bias,
        key_bias,
        value_bias,
        output_weight,
        feedforward_gain,
        router_weight,
        shared_switch,
        shared_gate,
        shared_up,
        shared_down,
    ) = (
        lax.all_gather(attention_gain, "ep", axis=0, tiled=True),
        lax.all_gather(query_weight, "ep", axis=0, tiled=True),
        lax.all_gather(key_weight, "ep", axis=0, tiled=True),
        lax.all_gather(value_weight, "ep", axis=0, tiled=True),
        lax.all_gather(query_bias, "ep", axis=1, tiled=True),
        lax.all_gather(key_bias, "ep", axis=1, tiled=True),
        lax.all_gather(value_bias, "ep", axis=1, tiled=True),
        lax.all_gather(output_weight, "ep", axis=1, tiled=True),
        lax.all_gather(feedforward_gain, "ep", axis=0, tiled=True),
        lax.all_gather(router_weight, "ep", axis=0, tiled=True),
        lax.all_gather(shared_switch, "ep", axis=0, tiled=True),
        lax.all_gather(shared_gate, "ep", axis=0, tiled=True),
        lax.all_gather(shared_up, "ep", axis=0, tiled=True),
        lax.all_gather(shared_down, "ep", axis=1, tiled=True),
    )
    slot_count = tokens.shape[0]
    model_width = tokens.shape[1]
    top_count = routes.shape[1]
    experts = router_weight.shape[1]
    heads_here = query_bias.shape[0]
    head_size = query_bias.shape[1]
    owners = lax.axis_size("ep")
    per_owner = expert_gate.shape[0]
    capacity = 3 * slot_count * top_count // (2 * experts)
    seq_length = lengths[0]
    positions = jnp.arange(slot_count, dtype=jnp.int32)
    live_rows = (positions < seq_length).astype(single_float32)
    inputs = tokens.astype(single_float32)
    scale_one = lax.rsqrt(jnp.mean(inputs * inputs, -1, keepdims=True) + epsilon)
    normed_one = inputs * scale_one
    attn_in = (normed_one * attention_gain.astype(single_float32)).astype(brain_float16)
    query_pre = jnp.dot(
        attn_in, query_weight, preferred_element_type=single_float32
    ) + query_bias.reshape(-1).astype(single_float32)
    key_pre = jnp.dot(
        attn_in, key_weight, preferred_element_type=single_float32
    ) + key_bias.reshape(-1).astype(single_float32)
    value_pre = jnp.dot(
        attn_in, value_weight, preferred_element_type=single_float32
    ) + value_bias.reshape(-1).astype(single_float32)
    cosine, sine_table = rotation_tables(slot_count, head_size)
    head_shape = (slot_count, heads_here, head_size)
    queries = rotate(query_pre.reshape(head_shape), cosine, sine_table).astype(brain_float16)
    key_heads = rotate(key_pre.reshape(head_shape), cosine, sine_table).astype(brain_float16)
    value_heads = value_pre.astype(brain_float16).reshape(head_shape)
    score_scale = head_size ** (-0.5)
    keep_mask = (positions[None, :] <= positions[:, None]) & (positions[None, :] < seq_length)
    scores = (
        jnp.einsum("shd,thd->hst", queries, key_heads, preferred_element_type=single_float32)
        * score_scale
    )
    scores = jnp.where(keep_mask[None], scores, -1e30)
    top_score = jnp.max(scores, -1, keepdims=True)
    exp_scores = jnp.exp(scores - top_score)
    row_total = jnp.sum(exp_scores, -1, keepdims=True)
    attn_probs = exp_scores / row_total
    log_total = top_score + jnp.log(row_total)
    mixed_heads = (
        jnp.einsum(
            "hst,thd->shd",
            attn_probs.astype(brain_float16),
            value_heads,
            preferred_element_type=single_float32,
        )
        .astype(brain_float16)
        .reshape(slot_count, -1)
    )
    attn_out = lax.psum(
        jnp.dot(mixed_heads, output_weight, preferred_element_type=single_float32), "tp"
    )
    hidden_state = inputs + attn_out
    scale_two = lax.rsqrt(jnp.mean(hidden_state * hidden_state, -1, keepdims=True) + epsilon)
    normed_two = hidden_state * scale_two
    mlp_in = (normed_two * feedforward_gain.astype(single_float32)).astype(brain_float16)
    logits = jnp.dot(mlp_in, router_weight, preferred_element_type=single_float32)
    top_logit = jnp.max(logits, -1, keepdims=True)
    exp_logits = jnp.exp(logits - top_logit)
    router_probs = exp_logits / jnp.sum(exp_logits, -1, keepdims=True)
    expert_ids = jnp.arange(experts, dtype=jnp.int32)
    chosen = (routes[:, :, None] == expert_ids[None, None, :]).astype(single_float32)
    gate_values = jnp.sum(chosen * router_probs[:, None, :], -1)
    expert_counts = jnp.sum(live_rows[:, None] * jnp.sum(chosen, 1), 0)
    prob_sums = jnp.sum(live_rows[:, None] * router_probs, 0)
    expert_counts, prob_sums, live_total = lax.psum(
        (expert_counts, prob_sums, jnp.sum(live_rows)), "ep"
    )
    aux_loss = experts * jnp.sum(expert_counts / live_total * prob_sums / live_total)
    flat_ids = routes.reshape(-1)
    flat_hot = (flat_ids[:, None] == expert_ids[None, :]).astype(jnp.int32)
    slot_rank = jnp.sum((jnp.cumsum(flat_hot, 0) - flat_hot) * flat_hot, 1)
    slot_index = flat_ids * capacity + slot_rank
    row_count = slot_count * top_count
    slot_table = (
        jnp.full((experts * capacity,), row_count, jnp.int32)
        .at[slot_index]
        .set(jnp.arange(row_count, dtype=jnp.int32))
    )
    send_shape = (owners, per_owner * capacity, model_width)
    grid_shape = (owners, per_owner, capacity, model_width)
    padded_in = jnp.concatenate([mlp_in, jnp.zeros((1, model_width), brain_float16)], 0)
    send_buffer = padded_in[slot_table // top_count]
    gate_matrix, up_weight_matrix, down_matrix = (expert_gate, expert_up, expert_down)
    received_rows = send_rows(send_buffer.reshape(send_shape)).reshape(grid_shape)
    gate_hidden = jnp.einsum(
        "necd,edf->necf", received_rows, gate_matrix, preferred_element_type=single_float32
    )
    up_hidden = jnp.einsum(
        "necd,edf->necf", received_rows, up_weight_matrix, preferred_element_type=single_float32
    )
    activated_gate, slope_gate = silu_parts(gate_hidden)
    inner_act = (activated_gate * up_hidden).astype(brain_float16)
    expert_part = jnp.einsum(
        "necf,efd->necd", inner_act, down_matrix, preferred_element_type=single_float32
    )
    returned = send_home(expert_part.reshape(send_shape))
    returned = returned.reshape(experts * capacity, model_width)
    picked_rows = returned[slot_index].reshape(slot_count, top_count, model_width)
    mixture = jnp.sum(gate_values[:, :, None] * picked_rows.astype(single_float32), 1)
    share_gate_pre = jnp.dot(mlp_in, shared_gate, preferred_element_type=single_float32)
    share_up_pre = jnp.dot(mlp_in, shared_up, preferred_element_type=single_float32)
    share_act, share_slope = silu_parts(share_gate_pre)
    shared_inner = (share_act * share_up_pre).astype(brain_float16)
    shared_out = lax.psum(
        jnp.dot(shared_inner, shared_down, preferred_element_type=single_float32).astype(
            jnp.bfloat16
        ),
        "tp",
    ).astype(jnp.float32)
    switch_logit = jnp.dot(mlp_in, shared_switch, preferred_element_type=single_float32)
    switch = lax.logistic(switch_logit)
    block_result = hidden_state + mixture + switch[:, None] * shared_out
    output = block_result.astype(brain_float16)
    grad_out = cotangent.astype(single_float32) * live_rows[:, None]
    grad_share = (grad_out * switch[:, None]).astype(brain_float16)
    grad_switch = (jnp.sum(grad_out * shared_out, -1) * switch * (1.0 - switch)).astype(
        brain_float16
    )
    shared_down_grad = jnp.dot(shared_inner.T, grad_share, preferred_element_type=single_float32)
    grad_shared_inner = jnp.dot(grad_share, shared_down.T, preferred_element_type=single_float32)
    grad_sgate = (grad_shared_inner * share_up_pre * share_slope).astype(brain_float16)
    grad_sup = (grad_shared_inner * share_act).astype(brain_float16)
    shared_gate_grad = jnp.dot(mlp_in.T, grad_sgate, preferred_element_type=single_float32)
    shared_up_grad = jnp.dot(mlp_in.T, grad_sup, preferred_element_type=single_float32)
    shared_switch_grad = jnp.dot(grad_switch, mlp_in, preferred_element_type=single_float32)
    shared_back = lax.psum(
        (
            jnp.dot(grad_sgate, shared_gate.T, preferred_element_type=single_float32)
            + jnp.dot(grad_sup, shared_up.T, preferred_element_type=single_float32)
        ).astype(jnp.bfloat16),
        "tp",
    ).astype(jnp.float32)
    gate_grad = jnp.sum(grad_out[:, None, :] * picked_rows.astype(single_float32), -1)
    grad_rows = (
        (gate_values[:, :, None] * grad_out[:, None, :])
        .astype(brain_float16)
        .reshape(row_count, model_width)
    )
    padded_grad = jnp.concatenate([grad_rows, jnp.zeros((1, model_width), brain_float16)], 0)
    grad_buffer = padded_grad[slot_table]
    grad_received = send_rows(grad_buffer.reshape(send_shape)).reshape(grid_shape)
    expert_inner_gradient = jnp.einsum(
        "necd,efd->necf", grad_received, down_matrix, preferred_element_type=single_float32
    )
    grad_egate = (expert_inner_gradient * up_hidden * slope_gate).astype(brain_float16)
    expert_up_partial = (expert_inner_gradient * activated_gate).astype(brain_float16)
    expert_down_grad = jnp.einsum(
        "necf,necd->efd", inner_act, grad_received, preferred_element_type=single_float32
    )
    expert_gate_grad = jnp.einsum(
        "uxvp,uxvh->xph", received_rows, grad_egate, preferred_element_type=single_float32
    )
    expert_up_gradient = jnp.einsum(
        "uxvp,uxvh->xph", received_rows, expert_up_partial, preferred_element_type=single_float32
    )
    grad_back_rows = jnp.einsum(
        "kqib,qzb->kqiz", grad_egate, gate_matrix, preferred_element_type=single_float32
    ) + jnp.einsum(
        "kqib,qzb->kqiz", expert_up_partial, up_weight_matrix, preferred_element_type=single_float32
    )
    home_grad = send_home(grad_back_rows.reshape(send_shape))
    home_grad = home_grad.reshape(experts * capacity, model_width)
    expert_back = jnp.sum(
        home_grad[slot_index].reshape(slot_count, top_count, model_width).astype(single_float32), 1
    )
    grad_probs = (
        jnp.sum(chosen * gate_grad[:, :, None], 1)
        + aux_weight
        * experts
        * (expert_counts / (live_total * live_total))[None, :]
        * live_rows[:, None]
    )
    grad_logits = (
        router_probs * (grad_probs - jnp.sum(router_probs * grad_probs, -1, keepdims=True))
    ).astype(brain_float16)
    router_weight_grad = jnp.dot(mlp_in.T, grad_logits, preferred_element_type=single_float32)
    grad_mlp_in = (
        shared_back
        + expert_back
        + jnp.dot(grad_logits, router_weight.T, preferred_element_type=single_float32)
        + grad_switch.astype(single_float32)[:, None]
        * shared_switch.astype(single_float32)[None, :]
    )
    grad_norm_two = grad_mlp_in * feedforward_gain.astype(single_float32)
    feedforward_gain_grad = jnp.sum(grad_mlp_in * normed_two, 0)
    grad_hidden = grad_out + scale_two * (
        grad_norm_two - normed_two * jnp.mean(grad_norm_two * normed_two, -1, keepdims=True)
    )
    grad_branch = grad_hidden.astype(brain_float16)
    output_weight_grad = jnp.dot(mixed_heads.T, grad_branch, preferred_element_type=single_float32)
    grad_mixed = (
        jnp.dot(grad_branch, output_weight.T, preferred_element_type=single_float32)
        .astype(brain_float16)
        .reshape(head_shape)
    )
    grad_weights = jnp.einsum(
        "shd,thd->hst", grad_mixed, value_heads, preferred_element_type=single_float32
    )
    scores_again = (
        jnp.einsum("shd,thd->hst", queries, key_heads, preferred_element_type=single_float32)
        * score_scale
    )
    scores_again = jnp.where(keep_mask[None], scores_again, -1e30)
    probs_again = jnp.exp(scores_again - log_total)
    row_delta = jnp.sum(probs_again * grad_weights, -1, keepdims=True)
    grad_scores = (probs_again * (grad_weights - row_delta)).astype(brain_float16)
    grad_value = (
        jnp.einsum(
            "hst,shd->thd",
            probs_again.astype(brain_float16),
            grad_mixed,
            preferred_element_type=single_float32,
        )
        .astype(brain_float16)
        .reshape(slot_count, -1)
    )
    grad_queries = (
        jnp.einsum("hst,thd->shd", grad_scores, key_heads, preferred_element_type=single_float32)
        * score_scale
    )
    grad_keys = (
        jnp.einsum("hst,shd->thd", grad_scores, queries, preferred_element_type=single_float32)
        * score_scale
    )
    grad_query = (
        rotate_back(grad_queries, cosine, sine_table).astype(brain_float16).reshape(slot_count, -1)
    )
    grad_key = (
        rotate_back(grad_keys, cosine, sine_table).astype(brain_float16).reshape(slot_count, -1)
    )
    query_weight_grad = jnp.dot(attn_in.T, grad_query, preferred_element_type=single_float32)
    key_weight_grad = jnp.dot(attn_in.T, grad_key, preferred_element_type=single_float32)
    value_weight_grad = jnp.dot(attn_in.T, grad_value, preferred_element_type=single_float32)
    query_bias_grad = jnp.sum(grad_query.astype(single_float32), 0).reshape(heads_here, head_size)
    key_bias_grad = jnp.sum(grad_key.astype(single_float32), 0).reshape(heads_here, head_size)
    value_bias_grad = jnp.sum(grad_value.astype(single_float32), 0).reshape(heads_here, head_size)
    grad_attn_in = lax.psum(
        (
            jnp.dot(grad_query, query_weight.T, preferred_element_type=single_float32)
            + jnp.dot(grad_key, key_weight.T, preferred_element_type=single_float32)
            + jnp.dot(grad_value, value_weight.T, preferred_element_type=single_float32)
        ).astype(jnp.bfloat16),
        "tp",
    ).astype(jnp.float32)
    grad_norm_one = grad_attn_in * attention_gain.astype(single_float32)
    attention_gain_grad = jnp.sum(grad_attn_in * normed_one, 0)
    tokens_grad = grad_hidden + scale_one * (
        grad_norm_one - normed_one * jnp.mean(grad_norm_one * normed_one, -1, keepdims=True)
    )
    reduced = (
        lax.psum_scatter(
            attention_gain_grad.astype(jnp.bfloat16), "ep", scatter_dimension=0, tiled=True
        ).astype(jnp.float32),
        lax.psum_scatter(
            query_weight_grad.astype(jnp.bfloat16), "ep", scatter_dimension=0, tiled=True
        ).astype(jnp.float32),
        lax.psum_scatter(
            key_weight_grad.astype(jnp.bfloat16), "ep", scatter_dimension=0, tiled=True
        ).astype(jnp.float32),
        lax.psum_scatter(
            value_weight_grad.astype(jnp.bfloat16), "ep", scatter_dimension=0, tiled=True
        ).astype(jnp.float32),
        lax.psum_scatter(
            query_bias_grad.astype(jnp.bfloat16), "ep", scatter_dimension=1, tiled=True
        ).astype(jnp.float32),
        lax.psum_scatter(
            key_bias_grad.astype(jnp.bfloat16), "ep", scatter_dimension=1, tiled=True
        ).astype(jnp.float32),
        lax.psum_scatter(
            value_bias_grad.astype(jnp.bfloat16), "ep", scatter_dimension=1, tiled=True
        ).astype(jnp.float32),
        lax.psum_scatter(
            output_weight_grad.astype(jnp.bfloat16), "ep", scatter_dimension=1, tiled=True
        ).astype(jnp.float32),
        lax.psum_scatter(
            feedforward_gain_grad.astype(jnp.bfloat16), "ep", scatter_dimension=0, tiled=True
        ).astype(jnp.float32),
        lax.psum_scatter(
            router_weight_grad.astype(jnp.bfloat16), "ep", scatter_dimension=0, tiled=True
        ).astype(jnp.float32),
        lax.psum_scatter(
            shared_switch_grad.astype(jnp.bfloat16), "ep", scatter_dimension=0, tiled=True
        ).astype(jnp.float32),
        lax.psum_scatter(
            shared_gate_grad.astype(jnp.bfloat16), "ep", scatter_dimension=0, tiled=True
        ).astype(jnp.float32),
        lax.psum_scatter(
            shared_up_grad.astype(jnp.bfloat16), "ep", scatter_dimension=0, tiled=True
        ).astype(jnp.float32),
        lax.psum_scatter(
            shared_down_grad.astype(jnp.bfloat16), "ep", scatter_dimension=1, tiled=True
        ).astype(jnp.float32),
    )
    return (
        output,
        aux_loss,
        expert_counts,
        tokens_grad,
        reduced[0],
        reduced[1],
        reduced[2],
        reduced[3],
        reduced[4],
        reduced[5],
        reduced[6],
        reduced[7],
        reduced[8],
        reduced[9],
        reduced[10],
        reduced[11],
        reduced[12],
        reduced[13],
        expert_gate_grad,
        expert_up_gradient,
        expert_down_grad,
    )


def solution(mesh):
    return jax.shard_map(
        shards,
        mesh=mesh,
        in_specs=(
            P("ep", None),
            P("ep"),
            P("ep", None),
            P("ep"),
            P("ep", "tp"),
            P("ep", "tp"),
            P("ep", "tp"),
            P("tp", "ep"),
            P("tp", "ep"),
            P("tp", "ep"),
            P("tp", "ep"),
            P("ep"),
            P("ep", None),
            P("ep"),
            P("ep", "tp"),
            P("ep", "tp"),
            P("tp", "ep"),
            P("ep", None, "tp"),
            P("ep", None, "tp"),
            P("ep", "tp", None),
            P("ep", None),
        ),
        out_specs=(
            P("ep", None),
            P(),
            P(),
            P("ep", None),
            P("ep"),
            P("ep", "tp"),
            P("ep", "tp"),
            P("ep", "tp"),
            P("tp", "ep"),
            P("tp", "ep"),
            P("tp", "ep"),
            P("tp", "ep"),
            P("ep"),
            P("ep", None),
            P("ep"),
            P("ep", "tp"),
            P("ep", "tp"),
            P("tp", "ep"),
            P("ep", None, "tp"),
            P("ep", None, "tp"),
            P("ep", "tp", None),
        ),
        check_vma=False,
    )
```

profile of v0, /device:TPU:0, one launch (start us, length us, event | category | flops | bytes accessed | tf_op | source)
XLA Modules:
  0.0 2834.0 jit_solution(7469661438798851311)
XLA Ops:
  105.5 24.2 all-gather.22.cloned.1.call-done
  188.2 101.7 %all-reduce.12.cloned.1.call-done = f32[512,2048]{1,0:T(8,128)} async-done(((f32[512,2048]{1,0:T(8,128)}), f32[512,2048]{1,0:T(8,128)}) %all-reduce.12.cloned.1.call-update) | async-done | bytes 4194320 | tf_op jit(solution)/shard_map/psum | solution.py:162
  295.4 25.9 gather_fusion
  343.8 111.6 %all-gather.26.cloned.1.call-done = bf16[2048,1408]{1,0:T(8,128)(2,1)} async-done(((bf16[256,1408]{1,0:T(8,128)(2,1)}), bf16[2048,1408]{1,0:T(8,128)(2,1)}) %all-gather.26.cloned.1.call-update) | async-done | bytes 5767184 | tf_op jit(solution)/shard_map/all_gather | solution.py:106
  463.0 60.8 %all-gather.30.cloned.1.call-done = bf16[1408,2048]{1,0:T(8,128)(2,1)} async-done(((bf16[1408,256]{1,0:T(8,128)(2,1)}), bf16[1408,2048]{1,0:T(8,128)(2,1)}) %all-gather.30.cloned.1.call-update) | async-done | bytes 5767184 | tf_op jit(solution)/shard_map/all_gather | solution.py:108
  560.3 143.8 %all-reduce.16.cloned.1.call-done = (bf16[512,2048]{1,0:T(8,128)(2,1)}, bf16[512,2048]{1,0:T(8,128)(2,1)}) async-done(((bf16[512,2048]{1,0:T(8,128)(2,1)}, bf16[512,2048]{1,0:T(8,128)(2,1)}), (bf16[512,2048]{1,0:T(8,128)(2,1)}, bf16[512,2048]{1,0:T(8,128)(2,1)})) %all-reduce.16.cloned.1.call-update) | async-done | bytes 4194320 | tf_op jit(solution)/shard_map/psum | solution.py:217
  755.2 28.3 gather_fusion.2
  798.7 129.2 %all-to-all-done.2 = bf16[8,384,2048]{2,1,0:T(8,128)(2,1)} async-done(((bf16[8,384,2048]{2,1,0:T(8,128)(2,1)}), bf16[8,384,2048]{2,1,0:T(8,128)(2,1)}, u32[]{:S(2)}, u32[]{:S(2)}) %all-to-all-start.2) | async-done | bytes 12582944 | tf_op jit(solution)/shard_map/all_to_all | solution.py:43
  996.2 380.2 %reduce-scatter.20.cloned.1.call-done = f32[8,384,512]{2,1,0:T(8,128)} async-done(((f32[8,384,2048]{2,1,0:T(8,128)}), f32[8,384,512]{2,1,0:T(8,128)}) %reduce-scatter.20.cloned.1.call-update) | async-done | bytes 6291472 | tf_op jit(solution)/shard_map/reduce_scatter | solution.py:47
  1379.6 41.4 %all_to_all.20 = bf16[8,384,512]{2,1,0:T(8,128)(2,1)} all-to-all(bf16[8,384,512]{2,1,0:T(8,128)(2,1)S(1)} %convert_element_type.294), channel_id=1, replica_groups=mesh['ep'=8,'tp'=4] {'ep'}, dimensions={0} | all-to-all | bytes 6291456 | tf_op jit(solution)/shard_map/all_to_all | solution.py:50
  1421.1 374.0 %reduce-scatter.22.cloned.1.call-done = f32[8,384,512]{2,1,0:T(8,128)} async-done(((f32[8,384,2048]{2,1,0:T(8,128)}), f32[8,384,512]{2,1,0:T(8,128)}) %reduce-scatter.22.cloned.1.call-update) | async-done | bytes 6291472 | tf_op jit(solution)/shard_map/reduce_scatter | solution.py:47
  1798.2 41.5 %all_to_all.21 = bf16[8,384,512]{2,1,0:T(8,128)(2,1)} all-to-all(bf16[8,384,512]{2,1,0:T(8,128)(2,1)S(1)} %convert_element_type.312), channel_id=1, replica_groups=mesh['ep'=8,'tp'=4] {'ep'}, dimensions={0} | all-to-all | bytes 6291456 | tf_op jit(solution)/shard_map/all_to_all | solution.py:50
  1862.6 154.1 %all-gather.24.cloned.1.call-done = bf16[8,384,2048]{2,1,0:T(8,128)(2,1)} async-done(((bf16[8,384,512]{2,1,0:T(8,128)(2,1)}), bf16[8,384,2048]{2,1,0:T(8,128)(2,1)}) %all-gather.24.cloned.1.call-update) | async-done | bytes 12582928 | tf_op jit(solution)/shard_map/all_gather | solution.py:39
  2016.7 22.5 gather_fusion.1
  2090.6 144.1 %all-gather.32.cloned.1.call-done = bf16[8,384,2048]{2,1,0:T(8,128)(2,1)} async-done(((bf16[8,384,512]{2,1,0:T(8,128)(2,1)}), bf16[8,384,2048]{2,1,0:T(8,128)(2,1)}) %all-gather.32.cloned.1.call-update) | async-done | bytes 12582928 | tf_op jit(solution)/shard_map/all_gather | solution.py:39
  2234.6 22.5 gather_fusion.3
  2359.7 60.0 %reduce-scatter.34.cloned.1.call-done = bf16[256,1408]{1,0:T(8,128)(2,1)} async-done(((bf16[2048,1408]{1,0:T(8,128)(2,1)}), bf16[256,1408]{1,0:T(8,128)(2,1)}) %reduce-scatter.34.cloned.1.call-update) | async-done | bytes 720912 | tf_op jit(solution)/shard_map/reduce_scatter | solution.py:397
  2490.1 33.6 %reduce-scatter.40.cloned.1.call-done = bf16[16,4]{1,0:T(8,128)(2,1)} async-done(((bf16[128,4]{1,0:T(8,128)(2,1)}), bf16[16,4]{1,0:T(8,128)(2,1)}) %reduce-scatter.40.cloned.1.call-update) | async-done | bytes 144
  2525.1 33.5 %reduce-scatter.32.cloned.1.call-done = bf16[256,8]{0,1:T(8,128)(2,1)} async-done(((bf16[2048,8]{0,1:T(8,128)(2,1)}), bf16[256,8]{0,1:T(8,128)(2,1)}) %reduce-scatter.32.cloned.1.call-update) | async-done | bytes 4112 | tf_op jit(solution)/shard_map/reduce_scatter | solution.py:391
  2559.9 87.9 %all-reduce.14.cloned.1.call-done = bf16[512,2048]{1,0:T(8,128)(2,1)} async-done(((bf16[512,2048]{1,0:T(8,128)(2,1)}), bf16[512,2048]{1,0:T(8,128)(2,1)}) %all-reduce.14.cloned.1.call-update) | async-done | bytes 2097168 | tf_op jit(solution)/shard_map/psum | solution.py:350
  2650.6 23.8 all-reduce.6
  2693.0 42.6 %reduce-scatter.28.cloned.1.call-done = bf16[256,512]{1,0:T(8,128)(2,1)} async-done(((bf16[2048,512]{1,0:T(8,128)(2,1)}), bf16[256,512]{1,0:T(8,128)(2,1)}) %reduce-scatter.28.cloned.1.call-update) | async-done | bytes 262160 | tf_op jit(solution)/shard_map/reduce_scatter | solution.py:373
  2737.5 42.5 %reduce-scatter.26.cloned.1.call-done = bf16[256,512]{1,0:T(8,128)(2,1)} async-done(((bf16[2048,512]{1,0:T(8,128)(2,1)}), bf16[256,512]{1,0:T(8,128)(2,1)}) %reduce-scatter.26.cloned.1.call-update) | async-done | bytes 262160 | tf_op jit(solution)/shard_map/reduce_scatter | solution.py:370
  2781.8 42.6 %reduce-scatter.24.cloned.1.call-done = bf16[256,512]{1,0:T(8,128)(2,1)} async-done(((bf16[2048,512]{1,0:T(8,128)(2,1)}), bf16[256,512]{1,0:T(8,128)(2,1)}) %reduce-scatter.24.cloned.1.call-update) | async-done | bytes 262160 | tf_op jit(solution)/shard_map/reduce_scatter | solution.py:367
  (394 shorter events, 642.0 us)
Async XLA Ops:
  9.4 120.3 %all-gather.22.cloned.1.call-start = ((), (), s32[]{:S(2)}) async-start(), calls=%async_computation.20 | async-start | bytes 2359296 | tf_op jit(solution)/shard_map/all_gather | solution.py:102
  10.0 279.9 %all-reduce.12.cloned.1.call-start = ((), (), s32[]{:S(2)}) async-start(), calls=%async_computation.21 | async-start | bytes 8388608 | tf_op jit(solution)/shard_map/psum | solution.py:162
  134.8 201.3 %all-gather.28.cloned.1.call-start = ((), (), s32[]{:S(2)}) async-start(), calls=%async_computation.25 | async-start | bytes 6488064 | tf_op jit(solution)/shard_map/all_gather | solution.py:107
  135.4 320.0 %all-gather.26.cloned.1.call-start = ((), (), s32[]{:S(2)}) async-start(), calls=%async_computation.24 | async-start | bytes 6488064 | tf_op jit(solution)/shard_map/all_gather | solution.py:106
  136.1 387.7 %all-gather.30.cloned.1.call-start = ((), (), s32[]{:S(2)}) async-start(), calls=%async_computation.26 | async-start | bytes 6488064 | tf_op jit(solution)/shard_map/all_gather | solution.py:108
  321.3 462.3 %all-to-all-start = ((bf16[8,384,2048]{2,1,0:T(8,128)(2,1)}), bf16[8,384,2048]{2,1,0:T(8,128)(2,1)}, u32[]{:S(2)}, u32[]{:S(2)}) async-start(bf16[8,384,2048]{2,1,0:T(8,128)(2,1)} %bitcast.241), calls=%async_computation | async-start | bytes 25165824 | tf_op jit(solution)/shard_map/all_to_all | solution.py:43
  326.8 377.3 %all-reduce.16.cloned.1.call-start = ((), (), s32[]{:S(2)}) async-start(), calls=%async_computation.41 | async-start | bytes 8388608 | tf_op jit(solution)/shard_map/psum | solution.py:217
  783.5 144.4 %all-to-all-start.2 = ((bf16[8,384,2048]{2,1,0:T(8,128)(2,1)}), bf16[8,384,2048]{2,1,0:T(8,128)(2,1)}, u32[]{:S(2)}, u32[]{:S(2)}) async-start(bf16[8,384,2048]{2,1,0:T(8,128)(2,1)} %bitcast.242), calls=%async_computation.3 | async-start | bytes 25165824 | tf_op jit(solution)/shard_map/all_to_all | solution.py:43
  788.9 587.5 %reduce-scatter.20.cloned.1.call-start = ((), (), s32[]{:S(2)}) async-start(), calls=%async_computation.22 | async-start | bytes 31457280 | tf_op jit(solution)/shard_map/reduce_scatter | solution.py:47
  964.8 830.2 %reduce-scatter.22.cloned.1.call-start = ((), (), s32[]{:S(2)}) async-start(), calls=%async_computation.27 | async-start | bytes 31457280 | tf_op jit(solution)/shard_map/reduce_scatter | solution.py:47
  996.2 1020.5 %all-gather.24.cloned.1.call-start = ((), (), s32[]{:S(2)}) async-start(), calls=%async_computation.23 | async-start | bytes 15728640 | tf_op jit(solution)/shard_map/all_gather | solution.py:39
  1421.0 813.6 %all-gather.32.cloned.1.call-start = ((), (), s32[]{:S(2)}) async-start(), calls=%async_computation.28 | async-start | bytes 15728640 | tf_op jit(solution)/shard_map/all_gather | solution.py:39
  1839.8 507.9 %reduce-scatter.38.cloned.1.call-start = ((), (), s32[]{:S(2)}) async-start(), calls=%async_computation.37 | async-start | bytes 6488064 | tf_op jit(solution)/shard_map/reduce_scatter | solution.py:403
  1846.5 510.8 %reduce-scatter.36.cloned.1.call-start = ((), (), s32[]{:S(2)}) async-start(), calls=%async_computation.36 | async-start | bytes 6488064 | tf_op jit(solution)/shard_map/reduce_scatter | solution.py:400
  1854.9 564.8 %reduce-scatter.34.cloned.1.call-start = ((), (), s32[]{:S(2)}) async-start(), calls=%async_computation.35 | async-start | bytes 6488064 | tf_op jit(solution)/shard_map/reduce_scatter | solution.py:397
  1861.8 605.9 %reduce-scatter.44.cloned.1.call-start = ((), (), s32[]{:S(2)}) async-start(), calls=%async_computation.40 | async-start | bytes 36864
  2317.5 171.3 %reduce-scatter.42.cloned.1.call-start = ((), (), s32[]{:S(2)}) async-start(), calls=%async_computation.39 | async-start | bytes 36864
  2321.8 202.0 %reduce-scatter.40.cloned.1.call-start = ((), (), s32[]{:S(2)}) async-start(), calls=%async_computation.38 | async-start | bytes 36864
  2322.6 236.0 %reduce-scatter.32.cloned.1.call-start = ((), (), s32[]{:S(2)}) async-start(), calls=%async_computation.34 | async-start | bytes 36864 | tf_op jit(solution)/shard_map/reduce_scatter | solution.py:391
  2323.7 324.1 %all-reduce.14.cloned.1.call-start = ((), (), s32[]{:S(2)}) async-start(), calls=%async_computation.29 | async-start | bytes 4194304 | tf_op jit(solution)/shard_map/psum | solution.py:350
  2331.4 359.8 %reduce-scatter.30.cloned.1.call-start = ((), (), s32[]{:S(2)}) async-start(), calls=%async_computation.33 | async-start | bytes 2359296 | tf_op jit(solution)/shard_map/reduce_scatter | solution.py:385
  2336.5 399.1 %reduce-scatter.28.cloned.1.call-start = ((), (), s32[]{:S(2)}) async-start(), calls=%async_computation.32 | async-start | bytes 2359296 | tf_op jit(solution)/shard_map/reduce_scatter | solution.py:373
  2341.3 438.7 %reduce-scatter.26.cloned.1.call-start = ((), (), s32[]{:S(2)}) async-start(), calls=%async_computation.31 | async-start | bytes 2359296 | tf_op jit(solution)/shard_map/reduce_scatter | solution.py:370
  2345.8 478.6 %reduce-scatter.24.cloned.1.call-start = ((), (), s32[]{:S(2)}) async-start(), calls=%async_computation.30 | async-start | bytes 2359296 | tf_op jit(solution)/shard_map/reduce_scatter | solution.py:367
  (91 other events, 3538.3 us)
Sparse Core Ops, SparseCore 0:
  9.9 30.4 all-gather.17
  42.3 27.7 all-gather.19
  101.6 28.0 all-gather.21
  134.9 154.9 all-reduce.11
  291.7 44.4 all-gather.27
  338.0 117.3 all-gather.25
  457.3 66.4 all-gather.29
  549.0 154.9 all-reduce.15
  965.0 411.3 reduce-scatter.19
  1378.8 416.1 reduce-scatter.21
  1796.4 220.1 all-gather.23
  2018.2 216.3 all-gather.31
  2237.9 57.0 reduce-scatter.37
  2298.3 59.0 reduce-scatter.35
  2360.7 58.9 reduce-scatter.33
  2422.5 31.3 reduce-scatter.43
  2457.4 31.3 reduce-scatter.41
  2492.3 31.3 reduce-scatter.39
  2527.2 31.3 reduce-scatter.31
  2561.5 86.1 all-reduce.13
  2651.0 40.1 reduce-scatter.29
  2694.5 41.0 reduce-scatter.27
  2738.8 41.1 reduce-scatter.25
  2783.3 41.0 reduce-scatter.23
  (1 shorter events, 27.7 us)
where the time goes:
time: 2850 us; the launch traced here: 2830 us
  waiting for transfers between devices  2040 us (72%)
  matrix products  224 us (8%)
  local copies, waits for them, and re-layouts  216 us (8%)
  blocking collectives  198 us (7%)
  other arithmetic  122 us (4%)
    reduce_scatter x2, waiting for transfers between devices, send_home(): lax.psum_scatter(partial_value, 'tp', scatter_dimension=2, tiled=True)  754 us
    all_gather x2, waiting for transfers between devices, join_features(): return lax.all_gather(arrived, 'tp', axis=2, tiled=True)  298 us
    psum x1, waiting for transfers between devices, shards(): lax.psum(jnp.dot(shared_inner, shared_down, preferred_element_type=single...  144 us
    all_to_all x2, waiting for transfers between devices, send_rows(): return lax.all_to_all(buffer, 'ep', split_axis=0, concat_axis=0, tiled=True)  129 us
    all_gather x1, waiting for transfers between devices, shards(): lax.all_gather(shared_gate, 'ep', axis=0, tiled=True)  112 us
    psum x1, waiting for transfers between devices, shards(): lax.psum(jnp.dot(mixed_heads, output_weight, preferred_element_type=singl...  102 us
    psum x1, waiting for transfers between devices, shards(): lax.psum((jnp.dot(grad_query, query_weight.T, preferred_element_type=sing...  87.9 us
    all_to_all x2, blocking collectives, send_home(): lax.all_to_all(summed_rows, 'ep', split_axis=0, concat_axis=0, tiled=True)  82.9 us
  transfers between devices with their start and end apart: 27, of which 23 were waited for; matrix products, arithmetic and copies ran while one was open for 18% of the time, Pallas kernels for 0%

commit v1 on v0

--- a/solution.py
+++ b/solution.py
@@ -51,7 +51,7 @@
     return join_features(arrived)
 
 
-def shards(
+def slot_shards(
     tokens,
     lengths,
     routes,
@@ -429,9 +429,373 @@
     )
 
 
+lane_width = 128
+
+
+def padded_size(units):
+    return -(-units // lane_width) * lane_width
+
+
+def pad_columns(matrix, width):
+    return jnp.pad(matrix, ((0, 0), (0, width - matrix.shape[1])))
+
+
+def dense_shards(
+    tokens,
+    lengths,
+    routes,
+    attention_gain,
+    query_weight,
+    key_weight,
+    value_weight,
+    query_bias,
+    key_bias,
+    value_bias,
+    output_weight,
+    feedforward_gain,
+    router_weight,
+    shared_switch,
+    shared_gate,
+    shared_up,
+    shared_down,
+    expert_gate,
+    expert_up,
+    expert_down,
+    cotangent,
+):
+    f32 = jnp.float32
+    bf16 = jnp.bfloat16
+    owners = lax.axis_size("ep")
+    my_expert = lax.axis_index("ep")
+    slot_count, model_width = tokens.shape
+    top_count = routes.shape[1]
+    experts = router_weight.shape[1]
+    heads_here, bias_cut = query_bias.shape
+    head_size = bias_cut * owners
+    head_width = heads_here * head_size
+    rows_here = query_weight.shape[0]
+    expert_units = expert_gate.shape[2]
+    shared_units = shared_gate.shape[1] // owners
+    expert_room = padded_size(expert_units)
+    shared_room = padded_size(shared_units)
+    all_tokens = owners * slot_count
+
+    packed = jnp.concatenate([query_weight, key_weight, value_weight, output_weight.T], 1)
+    packed = lax.all_gather(packed, "ep", axis=0, tiled=True)
+    qkv_weight = packed[:, : 3 * head_width]
+    output_back = packed[:, 3 * head_width :]
+
+    small = [
+        attention_gain,
+        feedforward_gain,
+        shared_switch,
+        router_weight.reshape(-1),
+        query_bias.reshape(-1),
+        key_bias.reshape(-1),
+        value_bias.reshape(-1),
+        routes.reshape(-1).astype(bf16),
+        (lengths // 256).astype(bf16),
+        (lengths % 256).astype(bf16),
+    ]
+    small_sizes = [piece.shape[0] for piece in small]
+    small = jnp.concatenate(small)
+    small = jnp.pad(small, (0, -small.shape[0] % 1024))
+    small = lax.all_gather(small[None], "ep", axis=0, tiled=True)
+    pieces = []
+    start = 0
+    for size in small_sizes:
+        pieces.append(small[:, start : start + size])
+        start += size
+    attn_gain = pieces[0].reshape(model_width).astype(f32)
+    ff_gain = pieces[1].reshape(model_width).astype(f32)
+    switch_weight = pieces[2].reshape(model_width)
+    router = pieces[3].reshape(model_width, experts)
+    biases = jnp.stack(pieces[4:7]).reshape(3, owners, heads_here, bias_cut)
+    biases = biases.transpose(0, 2, 1, 3).reshape(3 * head_width).astype(f32)
+    all_routes = pieces[7].reshape(all_tokens, top_count).astype(jnp.int32)
+    all_lengths = pieces[8].astype(f32) * 256 + pieces[9].astype(f32)
+    all_lengths = all_lengths.astype(jnp.int32).reshape(owners)
+
+    seq_length = lengths[0]
+    positions = jnp.arange(slot_count, dtype=jnp.int32)
+    live_rows = (positions < seq_length).astype(f32)
+    live_all = (positions[None, :] < all_lengths[:, None]).astype(f32).reshape(all_tokens)
+    live_total = jnp.sum(live_all)
+    expert_ids = jnp.arange(experts, dtype=jnp.int32)
+    chosen_all = jnp.sum((all_routes[:, :, None] == expert_ids).astype(f32), 1)
+    chosen = jnp.sum((routes[:, :, None] == expert_ids).astype(f32), 1)
+    expert_counts = jnp.sum(live_all[:, None] * chosen_all, 0)
+
+    grad_live = jnp.where(live_rows[:, None] > 0, cotangent, jnp.zeros_like(cotangent))
+    grad_out = grad_live.astype(f32)
+    grad_all = lax.all_gather(grad_live, "ep", axis=0, tiled=True)
+
+    weight_cuts = jnp.concatenate(
+        [
+            shared_gate.reshape(rows_here, owners, shared_units).transpose(1, 0, 2),
+            shared_up.reshape(rows_here, owners, shared_units).transpose(1, 0, 2),
+            shared_down.reshape(owners, shared_units, rows_here).transpose(0, 2, 1),
+        ],
+        2,
+    )
+    weight_cuts = lax.all_to_all(weight_cuts, "ep", split_axis=0, concat_axis=0, tiled=True)
+    weight_cuts = weight_cuts.reshape(model_width, 3 * shared_units)
+    gate_matrix = jnp.concatenate(
+        [
+            pad_columns(expert_gate[0], expert_room),
+            pad_columns(weight_cuts[:, :shared_units], shared_room),
+        ],
+        1,
+    )
+    up_matrix = jnp.concatenate(
+        [
+            pad_columns(expert_up[0], expert_room),
+            pad_columns(weight_cuts[:, shared_units : 2 * shared_units], shared_room),
+        ],
+        1,
+    )
+    down_matrix = jnp.concatenate(
+        [
+            jnp.pad(expert_down[0], ((0, expert_room - expert_units), (0, 0))),
+            pad_columns(weight_cuts[:, 2 * shared_units :], shared_room).T,
+        ],
+        0,
+    )
+    units = expert_room + shared_room
+
+    inputs = tokens.astype(f32)
+    scale_one = lax.rsqrt(jnp.mean(inputs * inputs, -1, keepdims=True) + epsilon)
+    normed_one = inputs * scale_one
+    attn_in = (normed_one * attn_gain).astype(bf16)
+    qkv_pre = jnp.dot(attn_in, qkv_weight, preferred_element_type=f32) + biases
+    cosine, sine_table = rotation_tables(slot_count, head_size)
+    head_shape = (slot_count, heads_here, head_size)
+    queries = rotate(qkv_pre[:, :head_width].reshape(head_shape), cosine, sine_table).astype(bf16)
+    key_heads = rotate(
+        qkv_pre[:, head_width : 2 * head_width].reshape(head_shape), cosine, sine_table
+    ).astype(bf16)
+    value_heads = qkv_pre[:, 2 * head_width :].astype(bf16).reshape(head_shape)
+    score_scale = head_size ** (-0.5)
+    keep_mask = (positions[None, :] <= positions[:, None]) & (positions[None, :] < seq_length)
+    scores = (
+        jnp.einsum("shd,thd->hst", queries, key_heads, preferred_element_type=f32) * score_scale
+    )
+    scores = jnp.where(keep_mask[None], scores, -1e30)
+    top_score = jnp.max(scores, -1, keepdims=True)
+    exp_scores = jnp.exp(scores - top_score)
+    attn_probs = exp_scores / jnp.sum(exp_scores, -1, keepdims=True)
+    probs_low = attn_probs.astype(bf16)
+    mixed_heads = (
+        jnp.einsum("hst,thd->shd", probs_low, value_heads, preferred_element_type=f32)
+        .astype(bf16)
+        .reshape(slot_count, head_width)
+    )
+    attn_out = lax.psum(
+        jnp.einsum("sh,dh->sd", mixed_heads, output_back, preferred_element_type=f32).astype(bf16),
+        "tp",
+    )
+    hidden_state = inputs + attn_out.astype(f32)
+    scale_two = lax.rsqrt(jnp.mean(hidden_state * hidden_state, -1, keepdims=True) + epsilon)
+    normed_two = hidden_state * scale_two
+    mlp_in = (normed_two * ff_gain).astype(bf16)
+    mlp_all = lax.all_gather(mlp_in, "ep", axis=0, tiled=True)
+
+    router_switch = jnp.concatenate([router, switch_weight[:, None]], 1)
+
+    def routing(rows):
+        logits = jnp.dot(rows, router_switch, preferred_element_type=f32)
+        return jax.nn.softmax(logits[:, :experts], axis=-1), lax.logistic(logits[:, experts])
+
+    router_probs, switch = routing(mlp_in)
+    probs_all, switch_all = routing(mlp_all)
+    prob_sums = jnp.sum(live_all[:, None] * probs_all, 0)
+    aux_loss = experts * jnp.sum(expert_counts / live_total * prob_sums / live_total)
+    mine = (expert_ids == my_expert).astype(f32)
+    gate_all = jnp.sum(chosen_all * probs_all * mine, 1)
+    in_expert = jnp.arange(units) < expert_room
+    row_weight = jnp.where(in_expert[None, :], gate_all[:, None], switch_all[:, None])
+
+    grad_units = jnp.einsum("td,fd->tf", grad_all, down_matrix, preferred_element_type=f32)
+    gate_pre = jnp.dot(mlp_all, gate_matrix, preferred_element_type=f32)
+    up_pre = jnp.dot(mlp_all, up_matrix, preferred_element_type=f32)
+    act, slope = silu_parts(gate_pre)
+    inner = act * up_pre
+    inner_weighted = (row_weight * inner).astype(bf16)
+    weighted_grad = row_weight * grad_units
+    grad_gate = (weighted_grad * up_pre * slope).astype(bf16)
+    grad_up = (weighted_grad * act).astype(bf16)
+    unit_products = inner * grad_units
+    gate_sum = jnp.sum(unit_products[:, :expert_room], -1)
+    switch_sum = jnp.sum(unit_products[:, expert_room:], -1)
+
+    result_part = jnp.dot(inner_weighted, down_matrix, preferred_element_type=f32).astype(bf16)
+    result_part = lax.psum_scatter(result_part, "ep", scatter_dimension=0, tiled=True)
+
+    extra_ids = jnp.arange(lane_width, dtype=jnp.int32)
+    extra = jnp.where(extra_ids == my_expert, gate_sum[:, None], 0.0) + jnp.where(
+        extra_ids == experts, switch_sum[:, None], 0.0
+    )
+    back_part = jnp.einsum(
+        "tf,df->td",
+        jnp.concatenate([grad_gate, grad_up], 1),
+        jnp.concatenate([gate_matrix, up_matrix], 1),
+        preferred_element_type=f32,
+    ).astype(bf16)
+    back_part = jnp.concatenate([back_part, extra.astype(bf16)], 1)
+    back_part = lax.psum_scatter(back_part, "ep", scatter_dimension=0, tiled=True)
+    back = lax.psum(back_part, "tp").astype(f32)
+    result_sum = lax.psum(result_part, "tp").astype(f32)
+    output = (hidden_state + result_sum).astype(bf16)
+
+    gate_weight_grad = jnp.einsum("td,tf->df", mlp_all, grad_gate, preferred_element_type=f32)
+    up_weight_grad = jnp.einsum("td,tf->df", mlp_all, grad_up, preferred_element_type=f32)
+    down_weight_grad = jnp.einsum(
+        "tf,td->fd", inner_weighted, grad_all, preferred_element_type=f32
+    )
+    shared_cut = slice(expert_room, expert_room + shared_units)
+    grad_cuts = jnp.concatenate(
+        [
+            gate_weight_grad[:, shared_cut].astype(bf16),
+            up_weight_grad[:, shared_cut].astype(bf16),
+            down_weight_grad[shared_cut].astype(bf16).T,
+        ],
+        1,
+    ).reshape(owners, rows_here, 3 * shared_units)
+    grad_cuts = lax.all_to_all(grad_cuts, "ep", split_axis=0, concat_axis=0, tiled=True)
+    grad_cuts = grad_cuts.reshape(owners, rows_here, 3, shared_units)
+    shared_gate_grad = grad_cuts[:, :, 0].transpose(1, 0, 2).reshape(shared_gate.shape).astype(f32)
+    shared_up_grad = grad_cuts[:, :, 1].transpose(1, 0, 2).reshape(shared_up.shape).astype(f32)
+    shared_down_grad = (
+        grad_cuts[:, :, 2].transpose(0, 2, 1).reshape(shared_down.shape).astype(f32)
+    )
+
+    gate_grad = back[:, model_width : model_width + experts]
+    grad_switch = (back[:, model_width + experts] * switch * (1.0 - switch)).astype(bf16)
+    grad_probs = (
+        chosen * gate_grad
+        + aux_weight
+        * experts
+        * (expert_counts / (live_total * live_total))[None, :]
+        * live_rows[:, None]
+    )
+    grad_logits = (
+        router_probs * (grad_probs - jnp.sum(router_probs * grad_probs, -1, keepdims=True))
+    ).astype(bf16)
+    grad_choices = jnp.concatenate([grad_logits, grad_switch[:, None]], 1)
+    choice_weight_grad = jnp.einsum("td,te->de", mlp_in, grad_choices, preferred_element_type=f32)
+    grad_mlp_in = back[:, :model_width] + jnp.einsum(
+        "te,de->td", grad_choices, router_switch, preferred_element_type=f32
+    )
+    grad_norm_two = grad_mlp_in * ff_gain
+    feedforward_gain_grad = jnp.sum(grad_mlp_in * normed_two, 0)
+    grad_hidden = grad_out + scale_two * (
+        grad_norm_two - normed_two * jnp.mean(grad_norm_two * normed_two, -1, keepdims=True)
+    )
+    grad_branch = grad_hidden.astype(bf16)
+    output_weight_grad = jnp.einsum(
+        "sd,sh->dh", grad_branch, mixed_heads, preferred_element_type=f32
+    )
+    grad_mixed = (
+        jnp.dot(grad_branch, output_back, preferred_element_type=f32)
+        .astype(bf16)
+        .reshape(head_shape)
+    )
+    grad_weights = jnp.einsum("shd,thd->hst", grad_mixed, value_heads, preferred_element_type=f32)
+    row_delta = jnp.sum(attn_probs * grad_weights, -1, keepdims=True)
+    grad_scores = (attn_probs * (grad_weights - row_delta)).astype(bf16)
+    grad_value = (
+        jnp.einsum("hst,shd->thd", probs_low, grad_mixed, preferred_element_type=f32)
+        .astype(bf16)
+        .reshape(slot_count, head_width)
+    )
+    grad_queries = (
+        jnp.einsum("hst,thd->shd", grad_scores, key_heads, preferred_element_type=f32)
+        * score_scale
+    )
+    grad_keys = (
+        jnp.einsum("hst,shd->thd", grad_scores, queries, preferred_element_type=f32) * score_scale
+    )
+    grad_query = rotate_back(grad_queries, cosine, sine_table).astype(bf16)
+    grad_key = rotate_back(grad_keys, cosine, sine_table).astype(bf16)
+    grad_qkv = jnp.concatenate(
+        [
+            grad_query.reshape(slot_count, head_width),
+            grad_key.reshape(slot_count, head_width),
+            grad_value,
+        ],
+        1,
+    )
+    qkv_weight_grad = jnp.einsum("td,th->dh", attn_in, grad_qkv, preferred_element_type=f32)
+    bias_grads = jnp.sum(grad_qkv.astype(f32), 0)
+    grad_attn_part = jnp.einsum("th,dh->td", grad_qkv, qkv_weight, preferred_element_type=f32)
+    attention_gain_part = jnp.sum(grad_attn_part * normed_one, 0)
+    grad_attn_in = lax.psum(grad_attn_part.astype(bf16), "tp").astype(f32)
+    grad_norm_one = grad_attn_in * attn_gain
+    tokens_grad = grad_hidden + scale_one * (
+        grad_norm_one - normed_one * jnp.mean(grad_norm_one * normed_one, -1, keepdims=True)
+    )
+
+    dense_grads = jnp.concatenate(
+        [qkv_weight_grad.astype(bf16), output_weight_grad.astype(bf16)], 1
+    )
+    dense_grads = lax.psum_scatter(dense_grads, "ep", scatter_dimension=0, tiled=True).astype(f32)
+    bias_grads = bias_grads.reshape(3, heads_here, owners, bias_cut).transpose(2, 0, 1, 3)
+    small_grads = jnp.concatenate(
+        [
+            attention_gain_part.reshape(owners, -1),
+            feedforward_gain_grad.reshape(owners, -1),
+            choice_weight_grad[:, experts].reshape(owners, -1),
+            choice_weight_grad[:, :experts].reshape(owners, -1),
+            bias_grads.reshape(owners, -1),
+        ],
+        1,
+    )
+    small_grads = jnp.pad(small_grads, ((0, 0), (0, -small_grads.shape[1] % 1024)))
+    small_grads = lax.all_to_all(small_grads, "ep", split_axis=0, concat_axis=0, tiled=True)
+    small_grads = jnp.sum(small_grads, 0)
+    attention_gain_grad = lax.psum(small_grads[:rows_here], "tp")
+    bias_at = (3 + experts) * rows_here
+    bias_rows = small_grads[bias_at : bias_at + 3 * heads_here * bias_cut]
+    bias_rows = bias_rows.reshape(3, heads_here, bias_cut)
+    return (
+        output,
+        aux_loss,
+        expert_counts,
+        tokens_grad,
+        attention_gain_grad,
+        dense_grads[:, :head_width],
+        dense_grads[:, head_width : 2 * head_width],
+        dense_grads[:, 2 * head_width : 3 * head_width],
+        bias_rows[0],
+        bias_rows[1],
+        bias_rows[2],
+        dense_grads[:, 3 * head_width : 4 * head_width].T,
+        small_grads[rows_here : 2 * rows_here],
+        small_grads[3 * rows_here : bias_at].reshape(rows_here, experts),
+        small_grads[2 * rows_here : 3 * rows_here],
+        shared_gate_grad,
+        shared_up_grad,
+        shared_down_grad,
+        gate_weight_grad[None, :, :expert_units],
+        up_weight_grad[None, :, :expert_units],
+        down_weight_grad[None, :expert_units],
+    )
+
+
+def layer_shards(*arrays):
+    routes, router_weight, expert_gate = arrays[2], arrays[12], arrays[17]
+    slot_count, top_count = routes.shape
+    experts = router_weight.shape[1]
+    capacity = 3 * slot_count * top_count // (2 * experts)
+    one_each = expert_gate.shape[0] == 1 and experts < lane_width
+    if one_each and 2 * capacity >= slot_count:
+        return dense_shards(*arrays)
+    return slot_shards(*arrays)
+
+
 def solution(mesh):
     return jax.shard_map(
-        shards,
+        layer_shards,
         mesh=mesh,
         in_specs=(
             P("ep", None),

time: 2850 us -> 1090 us (0.38)
  waiting for transfers between devices: 2040 us -> 661 us
  blocking collectives: 198 us -> 20.5 us
  local copies, waits for them, and re-layouts: 216 us -> 81.5 us
  other arithmetic: 122 us -> 76.2 us
    reduce_scatter x10 -> x3, waiting for transfers between devices: 991 us -> 250 us  [the longest x1 121 us: dense_shards(): lax.psum_scatter(back_part, 'ep', scatter_dimension=0, tiled=True)]
    all_gather x9 -> x3, waiting for transfers between devices: 529 us -> 173 us  [the longest x1 78.4 us: dense_shards(): mlp_all = lax.all_gather(mlp_in, 'ep', axis=0, tiled=True)]
    psum x3, waiting for transfers between devices: 333 us -> 188 us  [the longest x1 78.8 us: dense_shards(): lax.psum(jnp.einsum('sh,dh->sd', mixed_heads, output_back, preferred_elem...]
    gather x4 -> x0, local copies, waits for them, and re-layouts: 99.2 us -> none  [the longest x1 28.3 us: shards(): grad_buffer = padded_grad[slot_table]]
    all_to_all x2 -> x0, blocking collectives: 82.9 us -> none  [send_home(): lax.all_to_all(summed_rows, 'ep', split_axis=0, concat_axis=0, tiled=True)]
    all_to_all x2 -> x3, waiting for transfers between devices: 129 us -> 49.3 us  [the longest x1 34.1 us: dense_shards(): lax.all_to_all(weight_cuts, 'ep', split_axis=0, concat_axis=0, tiled=True)]
    unnamed x28 -> x9, waiting for transfers between devices: 58.2 us -> 0.15 us
    all_gather x7 -> x1, blocking collectives: 63.4 us -> 10.8 us  [dense_shards(): small = lax.all_gather(small[None], 'ep', axis=0, tiled=True)]
  transfers between devices with their start and end apart: 27 -> 12, of which waited for: 23 -> 11; matrix products, arithmetic and copies ran while one was open for 18% -> 20% of each run, Pallas kernels for 0% -> 0%
where the time goes in v1:
time: 1090 us; the launch traced here: 1080 us
  waiting for transfers between devices  661 us (61%)
  matrix products  207 us (19%)
  local copies, waits for them, and re-layouts  81.5 us (7%)
  other arithmetic  76.2 us (7%)
  blocking collectives  20.5 us (2%)
  between operations  19.1 us (2%)
  starting transfers between devices  12.4 us (1%)
    reduce_scatter x1, waiting for transfers between devices, dense_shards(): lax.psum_scatter(back_part, 'ep', scatter_dimension=0, tiled=True)  121 us
    reduce_scatter x1, waiting for transfers between devices, dense_shards(): lax.psum_scatter(result_part, 'ep', scatter_dimension=0, tiled=True)  93.9 us
    psum x1, waiting for transfers between devices, dense_shards(): lax.psum(jnp.einsum('sh,dh->sd', mixed_heads, output_back, preferred_elem...  78.8 us
    all_gather x1, waiting for transfers between devices, dense_shards(): mlp_all = lax.all_gather(mlp_in, 'ep', axis=0, tiled=True)  78.4 us
    psum x1, waiting for transfers between devices, dense_shards(): back = lax.psum(back_part, 'tp').astype(f32)  69.6 us
    all_gather x1, waiting for transfers between devices, dense_shards(): grad_all = lax.all_gather(grad_live, 'ep', axis=0, tiled=True)  55.1 us
    psum x1, waiting for transfers between devices, dense_shards(): result_sum = lax.psum(result_part, 'tp').astype(f32)  39.6 us
    all_gather x1, waiting for transfers between devices, dense_shards(): packed = lax.all_gather(packed, 'ep', axis=0, tiled=True)  39.6 us
  transfers between devices with their start and end apart: 12, of which 11 were waited for; matrix products, arithmetic and copies ran while one was open for 20% of the time, Pallas kernels for 0%

profile of v1, /device:TPU:0, one launch (start us, length us, event | category | flops | bytes accessed | tf_op | source)
XLA Modules:
  0.0 1077.9 jit_solution(6345713911967201000)
XLA Ops:
  14.4 10.8 all-gather
  31.7 39.6 %all-gather.5.cloned.1.call-done = bf16[2048,2048]{0,1:T(8,128)(2,1)} async-done(((bf16[256,2048]{0,1:T(8,128)(2,1)}), bf16[2048,2048]{0,1:T(8,128)(2,1)}) %all-gather.5.cloned.1.call-update) | async-done | bytes 8388624 | tf_op jit(solution)/shard_map/all_gather | solution.py:484
  108.1 78.8 %all-reduce.12.cloned.1.call-done = bf16[512,2048]{0,1:T(8,128)(2,1)} async-done(((bf16[512,2048]{0,1:T(8,128)(2,1)}), bf16[512,2048]{0,1:T(8,128)(2,1)}) %all-reduce.12.cloned.1.call-update) | async-done | bytes 2097168 | tf_op jit(solution)/shard_map/psum | solution.py:593
  212.0 34.1 %all-to-all-done = bf16[8,256,528]{1,2,0:T(8,128)(2,1)S(1)} async-done(((bf16[8,256,528]{1,2,0:T(8,128)(2,1)}), bf16[8,256,528]{1,2,0:T(8,128)(2,1)S(1)}, u32[]{:S(2)}, u32[]{:S(2)}) %all-to-all-start) | async-done | bytes 2162720 | tf_op jit(solution)/shard_map/all_to_all | solution.py:541
  248.9 55.1 %all-gather.9.cloned.1.call-done = bf16[4096,2048]{0,1:T(8,128)(2,1)} async-done(((bf16[512,2048]{0,1:T(8,128)(2,1)}), bf16[4096,2048]{0,1:T(8,128)(2,1)}) %all-gather.9.cloned.1.call-update) | async-done | bytes 16777232 | tf_op jit(solution)/shard_map/all_gather | solution.py:531
  304.1 16.9 %fusion.52 = f32[4096,640]{0,1:T(8,128)} fusion(bf16[4096,2048]{0,1:T(8,128)(2,1)} %all-gather.9.cloned.1.call-done, bf16[352,2048]{1,0:T(8,128)(2,1)S(1)} %bitcast.179, bf16[256,2048]{1,0:T(8,128)(2,1)S(1)} %pad_bitcast_fusion), kind=kOutput, calls=%fused_computation.97 | convolution fusion | flops 10745282560 | bytes 29753344 | tf_op jit(solution)/shard_map/td,fd->tf/dot_general | solution.py:618
  321.0 78.4 %all-gather.7.cloned.1.call-done = bf16[4096,2048]{0,1:T(8,128)(2,1)} async-done(((bf16[512,2048]{0,1:T(8,128)(2,1)}), bf16[4096,2048]{0,1:T(8,128)(2,1)}) %all-gather.7.cloned.1.call-update) | async-done | bytes 16777232 | tf_op jit(solution)/shard_map/all_gather | solution.py:601
  410.4 13.9 %fusion.39 = f32[4096,640]{0,1:T(8,128)} fusion(bf16[4096,2048]{0,1:T(8,128)(2,1)S(1)} %copy-done.7, bf16[2048,256]{0,1:T(8,128)(2,1)} %pad.33, bf16[2048,384]{0,1:T(8,128)(2,1)S(1)} %copy-done.21), kind=kOutput, calls=%fused_computation.72 | convolution fusion | flops 10742661120 | bytes 29884416 | tf_op jit(solution)/shard_map/dot_general | solution.py:620
  424.3 29.6 %multiply_convert_fusion.1 = (bf16[4096,640]{0,1:T(8,128)(2,1)}, f32[4096,640]{0,1:T(8,128)}, bf16[4096,640]{0,1:T(8,128)(2,1)}, bf16[4096,640]{0,1:T(8,128)(2,1)}) fusion(f32[4096,640]{0,1:T(8,128)} %fusion.39, f32[4096,640]{0,1:T(8,128)} %fusion.52, f32[4096]{0:T(1024)S(1)} %bitcast.176, f32[4096]{0:T(1024)S(1)} %get-tuple-element.152, ...), kind=kOutput, calls=%fused_computation.11 | convolution fusion | flops 10792468480 | bytes 66617984 | tf_op jit(solution)/shard_map/dot_general | solution.py:619
  459.5 26.9 %convolution_convert_fusion.1 = bf16[4096,2048]{0,1:T(8,128)(2,1)} fusion(bf16[4096,640]{0,1:T(8,128)(2,1)} %get-tuple-element.158, bf16[4096,640]{0,1:T(8,128)(2,1)} %get-tuple-element.156, bf16[2048,256]{0,1:T(8,128)(2,1)} %pad.33, bf16[2048,384]{0,1:T(8,128)(2,1)S(1)} %copy-done.21, bf16[2048,256]{0,1:T(8,128)(2,1)S(1)} %copy-done.27, ...), kind=kOutput, calls=%fused_computation.3 | convolution fusion | flops 21525168128 | bytes 32505856 | tf_op jit(solution)/shard_map/tf,df->td/dot_general | solution.py:638
  486.8 14.2 %pad_maximum_fusion = bf16[4096,2176]{0,1:T(8,128)(2,1)} fusion(bf16[4096,128]{0,1:T(8,128)(2,1)S(1)} %add_convert_fusion.1, bf16[4096,2048]{0,1:T(8,128)(2,1)} %convolution_convert_fusion.1), kind=kLoop, calls=%fused_computation.1 | loop fusion | flops 35651584 | bytes 35651584 | tf_op jit(solution)/shard_map/concatenate | solution.py:644
  501.1 121.1 %reduce-scatter.6.cloned.1.call-done = bf16[512,2176]{0,1:T(8,128)(2,1)} async-done(((bf16[4096,2176]{0,1:T(8,128)(2,1)}), bf16[512,2176]{0,1:T(8,128)(2,1)}) %reduce-scatter.6.cloned.1.call-update) | async-done | bytes 2228240 | tf_op jit(solution)/shard_map/reduce_scatter | solution.py:645
  622.2 18.4 %convolution_convert_fusion = bf16[4096,2048]{0,1:T(8,128)(2,1)} fusion(bf16[4096,640]{0,1:T(8,128)(2,1)} %get-tuple-element.159, bf16[352,2048]{1,0:T(8,128)(2,1)S(1)} %bitcast.180, bf16[256,2048]{1,0:T(8,128)(2,1)S(1)} %copy-done.26), kind=kOutput, calls=%fused_computation.2 | convolution fusion | flops 10753671168 | bytes 24510464 | tf_op jit(solution)/shard_map/dot_general | solution.py:631
  645.2 69.6 %all-reduce.14.cloned.1.call-done = bf16[512,2176]{0,1:T(8,128)(2,1)} async-done(((bf16[512,2176]{0,1:T(8,128)(2,1)}), bf16[512,2176]{0,1:T(8,128)(2,1)}) %all-reduce.14.cloned.1.call-update) | async-done | bytes 2228240 | tf_op jit(solution)/shard_map/psum | solution.py:646
  739.5 93.9 %reduce-scatter.4.cloned.1.call-done = bf16[512,2048]{0,1:T(8,128)(2,1)} async-done(((bf16[4096,2048]{0,1:T(8,128)(2,1)}), bf16[512,2048]{0,1:T(8,128)(2,1)}) %reduce-scatter.4.cloned.1.call-update) | async-done | bytes 2097168 | tf_op jit(solution)/shard_map/reduce_scatter | solution.py:632
  833.5 16.1 %fusion.125 = f32[2048,640]{0,1:T(8,128)S(1)} fusion(bf16[4096,2048]{0,1:T(8,128)(2,1)} %all-gather.7.cloned.1.call-done, bf16[4096,640]{0,1:T(8,128)(2,1)} %get-tuple-element.158), kind=kOutput, calls=%fused_computation.238 | convolution fusion | flops 10737418240 | bytes 27262976 | tf_op jit(solution)/shard_map/td,tf->df/dot_general | solution.py:651
  858.3 8.4 pad_maximum_fusion.1
  866.7 15.4 %fusion.124 = f32[2048,640]{0,1:T(8,128)S(1)} fusion(bf16[4096,2048]{0,1:T(8,128)(2,1)} %all-gather.7.cloned.1.call-done, bf16[4096,640]{0,1:T(8,128)(2,1)} %get-tuple-element.156), kind=kOutput, calls=%fused_computation.237 | convolution fusion | flops 10737418240 | bytes 27262976 | tf_op jit(solution)/shard_map/td,tf->df/dot_general | solution.py:650
  884.5 18.0 %fusion.126 = f32[640,2048]{1,0:T(8,128)} fusion(bf16[4096,640]{0,1:T(8,128)(2,1)} %get-tuple-element.159, bf16[4096,2048]{0,1:T(8,128)(2,1)} %all-gather.9.cloned.1.call-done), kind=kOutput, calls=%fused_computation.239 | convolution fusion | flops 10737418240 | bytes 27262976 | tf_op jit(solution)/shard_map/tf,td->fd/dot_general | solution.py:652
  922.2 15.3 %all-to-all-done.2 = bf16[8,256,528]{1,2,0:T(8,128)(2,1)} async-done(((bf16[8,256,528]{1,2,0:T(8,128)(2,1)}), bf16[8,256,528]{1,2,0:T(8,128)(2,1)}, u32[]{:S(2)}, u32[]{:S(2)}) %all-to-all-start.2) | async-done | bytes 2162720 | tf_op jit(solution)/shard_map/all_to_all | solution.py:664
  951.3 39.6 %all-reduce.16.cloned.1.call-done = (bf16[512,2048]{0,1:T(8,128)(2,1)}, bf16[512,2048]{0,1:T(8,128)(2,1)}) async-done(((bf16[512,2048]{0,1:T(8,128)(2,1)}, bf16[512,2048]{0,1:T(8,128)(2,1)}), (bf16[512,2048]{0,1:T(8,128)(2,1)}, bf16[512,2048]{0,1:T(8,128)(2,1)})) %all-reduce.16.cloned.1.call-update) | async-done | bytes 4194320 | tf_op jit(solution)/shard_map/psum | solution.py:647
  999.0 9.1 fusion.26
  1019.5 9.8 psum.39
  1029.3 35.4 %reduce-scatter.8.cloned.1.call-done = bf16[256,2048]{0,1:T(8,128)(2,1)} async-done(((bf16[2048,2048]{0,1:T(8,128)(2,1)}), bf16[256,2048]{0,1:T(8,128)(2,1)}) %reduce-scatter.8.cloned.1.call-update) | async-done | bytes 1048592 | tf_op jit(solution)/shard_map/reduce_scatter | solution.py:741
  (325 shorter events, 190.3 us)
Async XLA Ops:
  7.3 64.1 %all-gather.5.cloned.1.call-start = ((), (), s32[]{:S(2)}) async-start(), calls=%async_computation.6 | async-start | bytes 9437184 | tf_op jit(solution)/shard_map/all_gather | solution.py:484
  12.6 174.3 %all-reduce.12.cloned.1.call-start = ((), (), s32[]{:S(2)}) async-start(), calls=%async_computation.7 | async-start | bytes 4194304 | tf_op jit(solution)/shard_map/psum | solution.py:593
  28.8 160.6 %copy-start = (bf16[512,2048]{0,1:T(8,128)(2,1)}, bf16[512,2048]{0,1:T(8,128)(2,1)S(1)}, u32[]{:S(2)}) copy-start(bf16[512,2048]{0,1:T(8,128)(2,1)S(1)} %copy.251) | copy-start | bytes 6291460
  100.6 203.4 %all-gather.9.cloned.1.call-start = ((), (), s32[]{:S(2)}) async-start(), calls=%async_computation.10 | async-start | bytes 18874368 | tf_op jit(solution)/shard_map/all_gather | solution.py:531
  104.6 84.8 %copy-start.56 = (pred[512]{0:T(512)(128)(4,1)}, pred[512]{0:T(512)(128)(4,1)S(1)}, u32[]{:S(2)}) copy-start(pred[512]{0:T(512)(128)(4,1)S(1)} %broadcast_compare_fusion) | copy-start | bytes 1540
  107.7 291.7 %all-gather.7.cloned.1.call-start = ((), (), s32[]{:S(2)}) async-start(), calls=%async_computation.8 | async-start | bytes 18874368 | tf_op jit(solution)/shard_map/all_gather | solution.py:601
  108.1 83.9 %copy-start.41 = (f32[1,2,8,128]{3,1,2,0:T(2,128)}, f32[1,2,8,128]{3,1,2,0:T(2,128)S(1)}, u32[]{:S(2)}) copy-start(f32[1,2,8,128]{3,1,2,0:T(2,128)S(1)} %copy.315) | copy-start | bytes 24580
  195.3 50.8 %all-to-all-start = ((bf16[8,256,528]{1,2,0:T(8,128)(2,1)}), bf16[8,256,528]{1,2,0:T(8,128)(2,1)S(1)}, u32[]{:S(2)}, u32[]{:S(2)}) async-start(bf16[8,256,528]{1,2,0:T(8,128)(2,1)} %pad_maximum_fusion.2), calls=%async_computation | async-start | bytes 4325376 | tf_op jit(solution)/shard_map/all_to_all | solution.py:541
  199.0 423.2 %reduce-scatter.6.cloned.1.call-start = ((), (), s32[]{:S(2)}) async-start(), calls=%async_computation.11 | async-start | bytes 20054016 | tf_op jit(solution)/shard_map/reduce_scatter | solution.py:645
  199.3 200.1 %copy-start.39 = (bf16[1,1,8,256]{3,1,2,0:T(2,128)(2,1)}, bf16[1,1,8,256]{3,1,2,0:T(2,128)(2,1)S(1)}, u32[]{:S(2)}) copy-start(bf16[1,1,8,256]{3,1,2,0:T(2,128)(2,1)S(1)} %copy.316) | copy-start | bytes 12292
  200.5 198.9 %copy-start.31 = (bf16[2048,8]{0,1:T(8,128)(2,1)}, bf16[2048,8]{0,1:T(8,128)(2,1)S(1)}, u32[]{:S(2)}) copy-start(bf16[2048,8]{0,1:T(8,128)(2,1)S(1)} %copy.272) | copy-start | bytes 98308
  247.7 73.3 %copy-start.25 = (bf16[256,2048]{1,0:T(8,128)(2,1)}, bf16[256,2048]{1,0:T(8,128)(2,1)S(1)}, u32[]{:S(2)}) copy-start(bf16[256,2048]{1,0:T(8,128)(2,1)S(1)} %pad_bitcast_fusion) | copy-start | bytes 3145732
  501.0 121.2 %copy-start.26 = (bf16[256,2048]{1,0:T(8,128)(2,1)S(1)}, bf16[256,2048]{1,0:T(8,128)(2,1)}, u32[]{:S(2)}) copy-start(bf16[256,2048]{1,0:T(8,128)(2,1)} %copy-done.25) | copy-start | bytes 3145732
  501.0 121.2 %copy-start.67 = (bf16[1,352,2048]{2,1,0:T(8,128)(2,1)S(1)}, bf16[1,352,2048]{2,1,0:T(8,128)(2,1)}, u32[]{:S(2)}) copy-start(bf16[1,352,2048]{2,1,0:T(8,128)(2,1)} %param.40) | copy-start | bytes 4325380
  501.0 213.8 %all-reduce.14.cloned.1.call-start = ((), (), s32[]{:S(2)}) async-start(), calls=%async_computation.12 | async-start | bytes 4456448 | tf_op jit(solution)/shard_map/psum | solution.py:646
  622.2 211.3 %reduce-scatter.4.cloned.1.call-start = ((), (), s32[]{:S(2)}) async-start(), calls=%async_computation.9 | async-start | bytes 18874368 | tf_op jit(solution)/shard_map/reduce_scatter | solution.py:632
  640.7 350.2 %all-reduce.16.cloned.1.call-start = ((), (), s32[]{:S(2)}) async-start(), calls=%async_computation.14 | async-start | bytes 8388608 | tf_op jit(solution)/shard_map/psum | solution.py:647
  643.7 73.7 %copy-start.1 = (bf16[512,2048]{0,1:T(8,128)(2,1)S(1)}, bf16[512,2048]{0,1:T(8,128)(2,1)}, u32[]{:S(2)}) copy-start(bf16[512,2048]{0,1:T(8,128)(2,1)} %copy-done) | copy-start | bytes 6291460
  643.7 73.7 %copy-start.42 = (f32[1,2,8,128]{3,1,2,0:T(2,128)S(1)}, f32[1,2,8,128]{3,1,2,0:T(2,128)}, u32[]{:S(2)}) copy-start(f32[1,2,8,128]{3,1,2,0:T(2,128)} %copy-done.41) | copy-start | bytes 24580
  643.7 73.7 %copy-start.46 = (f32[512]{0:T(512)S(1)}, f32[512]{0:T(512)}, u32[]{:S(2)}) copy-start(f32[512]{0:T(512)} %copy-done.45) | copy-start | bytes 6148
  732.4 120.3 %copy-start.17 = (bf16[512,4,128]{0,2,1:T(8,128)(2,1)}, bf16[512,4,128]{0,2,1:T(8,128)(2,1)S(1)}, u32[]{:S(2)}) copy-start(bf16[512,4,128]{0,2,1:T(8,128)(2,1)S(1)} %get-tuple-element.182) | copy-start | bytes 1572868
  833.5 231.2 %reduce-scatter.8.cloned.1.call-start = ((), (), s32[]{:S(2)}) async-start(), calls=%async_computation.13 | async-start | bytes 9437184 | tf_op jit(solution)/shard_map/reduce_scatter | solution.py:741
  905.8 31.7 %all-to-all-start.2 = ((bf16[8,256,528]{1,2,0:T(8,128)(2,1)}), bf16[8,256,528]{1,2,0:T(8,128)(2,1)}, u32[]{:S(2)}, u32[]{:S(2)}) async-start(bf16[8,256,528]{1,2,0:T(8,128)(2,1)} %bitcast.142), calls=%async_computation.5 | async-start | bytes 4325376 | tf_op jit(solution)/shard_map/all_to_all | solution.py:664
  995.3 20.7 %all-to-all-start.1 = ((f32[8,1,3072]{2,1,0:T(1,128)}), f32[8,1,3072]{2,1,0:T(1,128)S(1)}, u32[]{:S(2)}, u32[]{:S(2)}) async-start(f32[8,1,3072]{2,1,0:T(1,128)} %copy.288), calls=%async_computation.3 | async-start | bytes 196608 | tf_op jit(solution)/shard_map/all_to_all | solution.py:754
  (61 other events, 432.9 us)
Sparse Core Ops, SparseCore 0:
  12.7 58.5 all-gather.4
  100.7 86.1 all-reduce.11
  188.8 115.2 all-gather.8
  306.4 93.0 all-gather.6
  501.1 120.9 reduce-scatter.5
  624.4 90.3 all-reduce.13
  718.4 115.0 reduce-scatter.3
  835.9 155.0 all-reduce.15
  994.4 70.2 reduce-scatter.7
